TPU v7x, 32 devices: a whole 2x2x4 slice. The times are simulated.
32 devices in a mesh: seq: 4 (over x, core), vocab: 8 (over z, y).
Axes of the slice: x: 2, y: 2, z: 4, core: 2. Of those that a mesh axis runs over, the one named last changes fastest.
Arguments:
- hidden: bfloat16 [512, 4608], P('seq', 'vocab'), may hold values from -6 to 6
- norm_gain: float32 [4608], replicated, may hold values from -1.5 to 1.5
- unembed: bfloat16 [256000, 4608], P(('seq', 'vocab')), may hold values from -0.375 to 0.375
- targets: int32 [512], P('seq'), may hold values from 0 to 255999
Outputs:
- log_prob: float32 [512], P('seq')
- entropy: float32 [512], P('seq')
All inputs are finite; a program needn't handle non-finite values.
Results may differ from a plain program's by a relative error of at most 0.0012.
Values may be sent and summed in bfloat16 or wider, within the bound.
A program may use at most 128 MiB of HBM per device.

v0:
```python
import jax
import jax.numpy as jnp
from jax import lax
from jax.sharding import PartitionSpec as P

softcap = 30.0
epsilon = 1e-06


def token_stats(logits, target_rows, first):
    capped = softcap * jnp.tanh(logits / softcap)
    weights = jnp.exp(capped - softcap)
    columns = first + lax.broadcasted_iota(jnp.int32, logits.shape, 1)
    chosen = jnp.where(columns == target_rows[:, None], capped, 0.0)
    return jnp.stack(
        [jnp.sum(weights, axis=1), jnp.sum(weights * capped, axis=1), jnp.sum(chosen, axis=1)]
    )


def on_device(hidden, norm_gain, unembed, targets):
    vocab_rows = unembed.shape[0]
    own_tokens = hidden.shape[0]
    first = lax.axis_index(("seq", "vocab")) * vocab_rows
    all_targets = lax.all_gather(targets, "seq", axis=0, tiled=True)
    rows = lax.all_gather(hidden, "vocab", axis=1, tiled=True).astype(jnp.float32)
    scale = lax.rsqrt(jnp.mean(rows * rows, axis=1, keepdims=True) + epsilon)
    normed = (rows * scale * (1.0 + norm_gain)).astype(jnp.bfloat16)
    logits = lax.dot_general(
        lax.all_gather(normed, "seq", axis=0, tiled=True),
        unembed,
        (((1,), (1,)), ((), ())),
        preferred_element_type=jnp.float32,
    )
    stats = token_stats(logits, all_targets, first)
    summed = lax.psum(stats, ("seq", "vocab"))
    mine = lax.dynamic_slice_in_dim(summed, lax.axis_index("seq") * own_tokens, own_tokens, 1)
    total = mine[0]
    moment = mine[1]
    chosen = mine[2]
    log_norm = softcap + jnp.log(total)
    return (chosen - log_norm, log_norm - moment / total)


def solution(mesh):
    return jax.shard_map(
        on_device,
        mesh=mesh,
        in_specs=(P("seq", "vocab"), P(), P(("seq", "vocab"), None), P("seq")),
        out_specs=(P("seq"), P("seq")),
        check_vma=False,
    )
```

profile of v0, /device:TPU:0, one launch (start us, length us, event | category | flops | bytes accessed | tf_op | source)
XLA Modules:
  0.0 194.3 jit_solution(5912990735798231276)
XLA Ops:
  7.2 0.0 all-gather.4.cloned.1.call-start
  7.2 0.7 all-gather.4.cloned.1.call-update
  7.9 0.0 all-gather.6.cloned.1.call-start
  7.9 0.7 broadcast_add_fusion
  8.7 45.4 %all-gather.4.cloned.1.call-done = bf16[128,4608]{0,1:T(8,128)(2,1)} async-done(((bf16[128,576]{0,1:T(8,128)(2,1)}), bf16[128,4608]{0,1:T(8,128)(2,1)}) %all-gather.4.cloned.1.call-update) | async-done | bytes 1179664 | tf_op jit(solution)/shard_map/all_gather | solution.py:25
  54.0 1.9 fusion.1
  55.9 3.9 %fusion.3 = bf16[128,4608]{0,1:T(8,128)(2,1)} fusion(bf16[128,4608]{0,1:T(8,128)(2,1)} %all-gather.4.cloned.1.call-done, f32[4608]{0:T(1024)S(1)} %broadcast_add_fusion, f32[128]{0:T(128)S(1)} %add_rsqrt_fusion), kind=kLoop, calls=%fused_computation.9 | loop fusion | flops 2359296 | bytes 2378240 | tf_op jit(solution)/shard_map/convert_element_type | solution.py:27
  59.8 0.0 all-gather.6.cloned.1.call-update
  59.8 5.2 %all-gather = s32[4,1,128]{2,1,0:T(1,128)S(1)} all-gather(s32[1,1,128]{2,1,0:T(1,128)} %bitcast.15), channel_id=1, replica_groups=mesh['seq'=4,'vocab'=8] {'seq'}, dimensions={0}, use_global_device_ids=true | all-gather | bytes 2560 | tf_op jit(solution)/shard_map/all_gather | solution.py:24
  65.0 31.7 %all-gather.6.cloned.1.call-done = bf16[512,4608]{0,1:T(8,128)(2,1)} async-done(((bf16[128,4608]{0,1:T(8,128)(2,1)}), bf16[512,4608]{0,1:T(8,128)(2,1)}) %all-gather.6.cloned.1.call-update) | async-done | bytes 4718608 | tf_op jit(solution)/shard_map/all_gather | solution.py:29
  96.7 50.8 %fusion = (f32[512]{0:T(512)S(1)}, f32[512]{0:T(512)S(1)}, f32[512]{0:T(512)S(1)}) fusion(s32[512]{0:T(512)S(1)} %bitcast.14, s32[8000]{0:T(1024)S(1)} %iota_add_fusion, bf16[8000,4608]{1,0:T(8,128)(2,1)} %param.6, bf16[512,4608]{0,1:T(8,128)(2,1)} %all-gather.6.cloned.1.call-done), kind=kOutput, calls=%fused_computation.3 | convolution fusion | flops 37785600000 | bytes 78486784 | tf_op jit(solution)/shard_map/dot_general | solution.py:28
  147.6 39.4 %psum.7 = f32[3,512]{1,0:T(4,128)S(1)} all-reduce(f32[3,512]{1,0:T(4,128)S(1)} %pad_maximum_fusion), channel_id=1, replica_groups=mesh['seq'=4,'vocab'=8] {'seq','vocab'}, use_global_device_ids=true, to_apply=%region_4.5 | all-reduce | flops 1536 | bytes 12288 | tf_op jit(solution)/shard_map/psum | solution.py:35
  186.9 0.5 subtract_bitcast_fusion
  (4 shorter events, 0.0 us)
Async XLA Ops:
  7.2 46.9 %all-gather.4.cloned.1.call-start = ((), (), s32[]{:S(2)}) async-start(), calls=%async_computation | async-start | bytes 1327104 | tf_op jit(solution)/shard_map/all_gather | solution.py:25
  7.9 88.8 %all-gather.6.cloned.1.call-start = ((), (), s32[]{:S(2)}) async-start(), calls=%async_computation.1 | async-start | bytes 5898240 | tf_op jit(solution)/shard_map/all_gather | solution.py:29
Sparse Core Ops, SparseCore 0:
  10.2 43.8 all-gather.3
  59.9 36.7 all-gather.5
where the time goes:
time: 195 us; the launch traced here: 194 us
  waiting for transfers between devices  77.7 us (40%)
  matrix products  50.8 us (26%)
  blocking collectives  44.6 us (23%)
  between operations  14.1 us (7%)
  other arithmetic  7.03 us (4%)
    dot_general x1, matrix products, on_device(): lax.dot_general(lax.all_gather(normed, 'seq', axis=0, tiled=True), unembe...  50.8 us
    all_gather x1, waiting for transfers between devices, on_device(): lax.all_gather(hidden, 'vocab', axis=1, tiled=True).astype(jnp.float32)  45.4 us
    psum x1, blocking collectives, on_device(): summed = lax.psum(stats, ('seq', 'vocab'))  39.4 us
    all_gather x1, waiting for transfers between devices, on_device(): lax.all_gather(normed, 'seq', axis=0, tiled=True)  31.7 us
    all_gather x1, blocking collectives, on_device(): all_targets = lax.all_gather(targets, 'seq', axis=0, tiled=True)  5.2 us
  transfers between devices with their start and end apart: 2, of which 2 were waited for; matrix products, arithmetic and copies ran while one was open for 0% of the time, Pallas kernels for 0%

commit v1 on v0

--- a/solution.py
+++ b/solution.py
@@ -32,7 +32,9 @@
         preferred_element_type=jnp.float32,
     )
     stats = token_stats(logits, all_targets, first)
-    summed = lax.psum(stats, ("seq", "vocab"))
+    summed = stats
+    for at in ("vocab", "seq"):
+        summed = lax.psum(summed, at)
     mine = lax.dynamic_slice_in_dim(summed, lax.axis_index("seq") * own_tokens, own_tokens, 1)
     total = mine[0]
     moment = mine[1]

time: 195 us -> 183 us (0.938)
  blocking collectives: 44.6 us -> 32.9 us
    psum x1 -> x2, blocking collectives: 39.4 us -> 27.7 us  [on_device(): summed = lax.psum(summed, at)]
where the time goes in v1:
time: 183 us
  waiting for transfers between devices  77.7 us (42%)
  matrix products  50.8 us (28%)
  blocking collectives  32.9 us (18%)
  between operations  14.1 us (8%)
  other arithmetic  7.03 us (4%)
    dot_general x1, matrix products, on_device(): lax.dot_general(lax.all_gather(normed, 'seq', axis=0, tiled=True), unembe...  50.8 us
    all_gather x1, waiting for transfers between devices, on_device(): lax.all_gather(hidden, 'vocab', axis=1, tiled=True).astype(jnp.float32)  45.4 us
    all_gather x1, waiting for transfers between devices, on_device(): lax.all_gather(normed, 'seq', axis=0, tiled=True)  31.7 us
    psum x2, blocking collectives, on_device(): summed = lax.psum(summed, at)  27.7 us
    all_gather x1, blocking collectives, on_device(): all_targets = lax.all_gather(targets, 'seq', axis=0, tiled=True)  5.2 us
    convert_element_type x1, other arithmetic, on_device(): normed = (rows * scale * (1.0 + norm_gain)).astype(jnp.bfloat16)  3.85 us
  transfers between devices with their start and end apart: 2, of which 2 were waited for; matrix products, arithmetic and copies ran while one was open for 0% of the time, Pallas kernels for 0%

profile of v1, /device:TPU:0, one launch (start us, length us, event | category | flops | bytes accessed | tf_op | source)
XLA Modules:
  0.0 182.7 jit_solution(4877591059456979763)
XLA Ops:
  7.2 0.0 all-gather.4.cloned.1.call-start
  7.2 0.7 all-gather.4.cloned.1.call-update
  7.9 0.0 all-gather.6.cloned.1.call-start
  7.9 0.7 broadcast_add_fusion
  8.7 45.4 %all-gather.4.cloned.1.call-done = bf16[128,4608]{0,1:T(8,128)(2,1)} async-done(((bf16[128,576]{0,1:T(8,128)(2,1)}), bf16[128,4608]{0,1:T(8,128)(2,1)}) %all-gather.4.cloned.1.call-update) | async-done | bytes 1179664 | tf_op jit(solution)/shard_map/all_gather | solution.py:25
  54.0 1.9 %fusion.1 = f32[128]{0:T(128)S(1)} fusion(bf16[128,4608]{0,1:T(8,128)(2,1)} %all-gather.4.cloned.1.call-done), kind=kLoop, calls=%fused_computation.7 | loop fusion | flops 1769344 | bytes 1180160 | tf_op jit(solution)/shard_map/reduce_sum | solution.py:26
  55.9 3.9 %fusion.3 = bf16[128,4608]{0,1:T(8,128)(2,1)} fusion(bf16[128,4608]{0,1:T(8,128)(2,1)} %all-gather.4.cloned.1.call-done, f32[4608]{0:T(1024)S(1)} %broadcast_add_fusion, f32[128]{0:T(128)S(1)} %add_rsqrt_fusion), kind=kLoop, calls=%fused_computation.9 | loop fusion | flops 2359296 | bytes 2378240 | tf_op jit(solution)/shard_map/convert_element_type | solution.py:27
  59.8 0.0 all-gather.6.cloned.1.call-update
  59.8 5.2 %all-gather = s32[4,1,128]{2,1,0:T(1,128)S(1)} all-gather(s32[1,1,128]{2,1,0:T(1,128)} %bitcast.15), channel_id=1, replica_groups=mesh['seq'=4,'vocab'=8] {'seq'}, dimensions={0}, use_global_device_ids=true | all-gather | bytes 2560 | tf_op jit(solution)/shard_map/all_gather | solution.py:24
  65.0 31.7 %all-gather.6.cloned.1.call-done = bf16[512,4608]{0,1:T(8,128)(2,1)} async-done(((bf16[128,4608]{0,1:T(8,128)(2,1)}), bf16[512,4608]{0,1:T(8,128)(2,1)}) %all-gather.6.cloned.1.call-update) | async-done | bytes 4718608 | tf_op jit(solution)/shard_map/all_gather | solution.py:29
  96.7 50.8 %fusion = (f32[512]{0:T(512)S(1)}, f32[512]{0:T(512)S(1)}, f32[512]{0:T(512)S(1)}) fusion(s32[512]{0:T(512)S(1)} %bitcast.14, s32[8000]{0:T(1024)S(1)} %iota_add_fusion, bf16[8000,4608]{1,0:T(8,128)(2,1)} %param.6, bf16[512,4608]{0,1:T(8,128)(2,1)} %all-gather.6.cloned.1.call-done), kind=kOutput, calls=%fused_computation.3 | convolution fusion | flops 37785600000 | bytes 78486784 | tf_op jit(solution)/shard_map/dot_general | solution.py:28
  147.6 21.6 %psum.14 = f32[3,512]{1,0:T(4,128)S(1)} all-reduce(f32[3,512]{1,0:T(4,128)S(1)} %pad_maximum_fusion), channel_id=1, replica_groups=mesh['seq'=4,'vocab'=8] {'vocab'}, use_global_device_ids=true, to_apply=%region_4.5 | all-reduce | flops 1536 | bytes 12288 | tf_op jit(solution)/shard_map/psum | solution.py:37
  169.2 6.1 %psum.15 = f32[3,512]{1,0:T(4,128)S(1)} all-reduce(f32[3,512]{1,0:T(4,128)S(1)} %psum.14), channel_id=1, replica_groups=mesh['seq'=4,'vocab'=8] {'seq'}, use_global_device_ids=true, to_apply=%region_5.6 | all-reduce | flops 1536 | bytes 12288 | tf_op jit(solution)/shard_map/psum | solution.py:37
  175.3 0.5 subtract_bitcast_fusion
  (4 shorter events, 0.0 us)
Async XLA Ops:
  7.2 46.9 %all-gather.4.cloned.1.call-start = ((), (), s32[]{:S(2)}) async-start(), calls=%async_computation | async-start | bytes 1327104 | tf_op jit(solution)/shard_map/all_gather | solution.py:25
  7.9 88.8 %all-gather.6.cloned.1.call-start = ((), (), s32[]{:S(2)}) async-start(), calls=%async_computation.1 | async-start | bytes 5898240 | tf_op jit(solution)/shard_map/all_gather | solution.py:29
Sparse Core Ops, SparseCore 0:
  10.2 43.8 all-gather.3
  59.9 36.7 all-gather.5
